TPU v7x, 32 devices: a whole 2x2x4 slice. The times are simulated.
32 devices in a mesh: dp: 4 (over x, core), fsdp: 8 (over z, y).
Axes of the slice: x: 2, y: 2, z: 4, core: 2. Of those that a mesh axis runs over, the one named last changes fastest.
Arguments:
- text_rows: bfloat16 [64, 512, 768], P(('dp', 'fsdp')), may hold values from -6 to 6
- visual_matrix: bfloat16 [768, 768], P('fsdp'), may hold values from -0.21875 to 0.21875
- batch_gain: bfloat16 [768], P('fsdp'), may hold values from 0.5 to 1.5
- batch_shift: bfloat16 [768], P('fsdp'), may hold values from -2.5 to 2.5
- attend_weight: bfloat16 [768, 2304], P('fsdp'), may hold values from -0.21875 to 0.21875
- merge_weight: bfloat16 [768, 768], P('fsdp'), may hold values from -1.75 to 1.75
- first_gain: bfloat16 [768], P('fsdp'), may hold values from 0.5 to 1.5
- first_shift: bfloat16 [768], P('fsdp'), may hold values from -2.5 to 2.5
- up_matrix: bfloat16 [768, 3072], P('fsdp'), may hold values from -0.21875 to 0.21875
- down_matrix: bfloat16 [3072, 768], P('fsdp'), may hold values from -0.109375 to 0.109375
- second_gain: bfloat16 [768], P('fsdp'), may hold values from 0.5 to 1.5
- second_shift: bfloat16 [768], P('fsdp'), may hold values from -2.5 to 2.5
- segment_counts: int32 [64], P(('dp', 'fsdp')), may hold values from 5 to 128, as said below
- segment_ids: int32 [64, 512], P(('dp', 'fsdp')), may hold values from -1 to 127, as said below
- padding_mask: int32 [64, 512], P(('dp', 'fsdp')), may hold values from 0 to 1, as said below
- cotangent: bfloat16 [64, 512, 768], P(('dp', 'fsdp')), may hold values from -6 to 6
Outputs:
- layer_output: float32 [64, 512, 768], P(('dp', 'fsdp'))
- text_gradient: float32 [64, 512, 768], P(('dp', 'fsdp'))
- visual_gradient: float32 [768, 768], P('fsdp')
- batch_gain_gradient: float32 [768], P('fsdp')
- batch_shift_gradient: float32 [768], P('fsdp')
- attend_gradient: float32 [768, 2304], P('fsdp')
- merge_gradient: float32 [768, 768], P('fsdp')
- first_gain_gradient: float32 [768], P('fsdp')
- first_shift_gradient: float32 [768], P('fsdp')
- up_gradient: float32 [768, 3072], P('fsdp')
- down_gradient: float32 [3072, 768], P('fsdp')
- second_gain_gradient: float32 [768], P('fsdp')
- second_shift_gradient: float32 [768], P('fsdp')
Inputs may be any that keep to these rules, and one draw needn't show every extreme that they name: On every device of dp+fsdp one of its documents has exactly 128 segments; segment_counts[d] is one more than the largest segment_ids in document d. `segment_ids`: A document's real rows come first and form segment_counts consecutive runs of one or more rows, numbered 0, 1, ... in order; padding rows hold -1. `padding_mask`: 1 exactly on the rows whose segment id is not -1, which are the first 256 or more rows of a document.
All inputs are finite; a program needn't handle non-finite values.
Results may differ from a plain program's by a relative error of at most 0.023.
The roundings to bfloat16 on the way count: a program that leaves them out, or rounds other values in their place, can miss the bound.
Values may be sent and summed in bfloat16 or wider, within the bound.
No kernel may reach another device: no remote copies, remote signals or barrier semaphores. Data moves between devices by JAX's collectives and lax.ppermute only.
A program may use at most 192 MiB of HBM per device.

v0:
```python
import jax
import jax.numpy as jnp
from jax import lax
from jax.sharding import PartitionSpec as P

HEADS = 12
SEGMAX = 128
eps_norm = 1e-05
eps_batch = 1e-05
masked_score = -1e30
highest_precision = lax.Precision.HIGHEST


def layer_norm(values, gain, shift):
    center = values - jnp.mean(values, axis=-1, keepdims=True)
    variance = jnp.mean(center * center, axis=-1, keepdims=True)
    return center * lax.rsqrt(variance + eps_norm) * gain + shift


def exact_gelu(values):
    return jax.nn.gelu(values, approximate=False)


def split_heads(packed):
    length = packed.shape[0]
    features = packed.shape[1] // 3
    head_size = features // HEADS
    queries = packed[:, :features].reshape(length, HEADS, head_size)
    keys_part = packed[:, features : 2 * features].reshape(length, HEADS, head_size)
    values_part = packed[:, 2 * features :].reshape(length, HEADS, head_size)
    return (queries, keys_part, values_part, head_size ** (-0.5))


def masked_scores(queries, keys_part, key_mask, scaling):
    scores = (
        jnp.einsum("qhe,khe->hqk", queries, keys_part, preferred_element_type=jnp.float32) * scaling
    )
    return jnp.where(key_mask[None, None, :] > 0, scores, masked_score)


def attend_doc(operands):
    packed, key_mask = operands
    queries, keys_part, values_part, scaling = split_heads(packed)
    scores = masked_scores(queries, keys_part, key_mask, scaling)
    top_score = jnp.max(scores, axis=-1, keepdims=True)
    unnormed = jnp.exp(scores - top_score)
    totals = jnp.sum(unnormed, axis=-1, keepdims=True)
    attention = unnormed / totals
    mixed = jnp.einsum(
        "hqk,khe->qhe",
        attention.astype(jnp.bfloat16),
        values_part,
        preferred_element_type=jnp.float32,
    )
    log_total = (top_score + jnp.log(totals))[..., 0]
    return (mixed.reshape(packed.shape[0], packed.shape[1] // 3).astype(jnp.bfloat16), log_total)


def attend_back(operands):
    packed, key_mask, log_total, delta_attended = operands
    queries, keys_part, values_part, scaling = split_heads(packed)
    length = packed.shape[0]
    features = packed.shape[1] // 3
    scores = masked_scores(queries, keys_part, key_mask, scaling)
    attention = jnp.exp(scores - log_total[..., None])
    delta_heads = delta_attended.reshape(length, HEADS, features // HEADS)
    delta_attention = jnp.einsum(
        "qhe,khe->hqk", delta_heads, values_part, preferred_element_type=jnp.float32
    )
    delta_scores = attention * (
        delta_attention - jnp.sum(attention * delta_attention, axis=-1, keepdims=True)
    )
    delta_low = delta_scores.astype(jnp.bfloat16)
    delta_queries = (
        jnp.einsum("hqk,khe->qhe", delta_low, keys_part, preferred_element_type=jnp.float32)
        * scaling
    )
    delta_keys = (
        jnp.einsum("hqk,qhe->khe", delta_low, queries, preferred_element_type=jnp.float32) * scaling
    )
    delta_values = jnp.einsum(
        "hqk,qhe->khe",
        attention.astype(jnp.bfloat16),
        delta_heads,
        preferred_element_type=jnp.float32,
    )
    merged = jnp.concatenate(
        [
            delta_queries.reshape(length, features),
            delta_keys.reshape(length, features),
            delta_values.reshape(length, features),
        ],
        axis=1,
    )
    return merged.astype(jnp.bfloat16)


def shards(
    text_rows,
    visual_matrix,
    batch_gain,
    batch_shift,
    attend_weight,
    merge_weight,
    first_gain,
    first_shift,
    up_matrix,
    down_matrix,
    second_gain,
    second_shift,
    segment_counts,
    segment_ids,
    padding_mask,
    cotangent,
):
    gathered = (
        lax.all_gather(visual_matrix, "fsdp", axis=0, tiled=True),
        lax.all_gather(batch_gain, "fsdp", axis=0, tiled=True),
        lax.all_gather(batch_shift, "fsdp", axis=0, tiled=True),
        lax.all_gather(attend_weight, "fsdp", axis=0, tiled=True),
        lax.all_gather(merge_weight, "fsdp", axis=0, tiled=True),
        lax.all_gather(first_gain, "fsdp", axis=0, tiled=True),
        lax.all_gather(first_shift, "fsdp", axis=0, tiled=True),
        lax.all_gather(up_matrix, "fsdp", axis=0, tiled=True),
        lax.all_gather(down_matrix, "fsdp", axis=0, tiled=True),
        lax.all_gather(second_gain, "fsdp", axis=0, tiled=True),
        lax.all_gather(second_shift, "fsdp", axis=0, tiled=True),
    )
    (
        gathered_visual_weight,
        full_batch_gain,
        full_batch_shift,
        full_attend,
        full_merge,
        full_first_gain,
        full_first_shift,
        gathered_up_weight,
        gathered_down_weight,
        full_second_gain,
        full_second_shift,
    ) = gathered
    features = text_rows.shape[2]
    slot_index = jnp.arange(SEGMAX)
    matches = segment_ids[:, :, None] == slot_index[None, None, :]
    onehot = matches.astype(jnp.bfloat16)
    onehot_wide = matches.astype(jnp.float32)
    divisor = jnp.maximum(jnp.sum(onehot_wide, axis=1), 1.0)[..., None]
    pooled_segments = (
        jnp.einsum("drs,drc->dsc", onehot, text_rows, preferred_element_type=jnp.float32) / divisor
    ).astype(jnp.bfloat16)
    visual_rows = jnp.einsum(
        "bil,ly->biy", pooled_segments, gathered_visual_weight, preferred_element_type=jnp.float32
    )
    valid_slot = (slot_index[None, :] < segment_counts[:, None]).astype(jnp.float32)[..., None]
    local_count = jnp.sum(segment_counts).astype(jnp.float32)
    masked_visual = valid_slot * visual_rows
    segment_total, visual_sum = lax.psum(
        (local_count, jnp.sum(masked_visual, axis=(0, 1))), ("dp", "fsdp")
    )
    batch_center = visual_sum / segment_total
    center = visual_rows - batch_center
    variance = (
        lax.psum(jnp.sum(valid_slot * center * center, axis=(0, 1)), ("dp", "fsdp")) / segment_total
    )
    inverse_spread = lax.rsqrt(variance + eps_batch)
    normed = center * inverse_spread
    embedded = (
        normed * full_batch_gain.astype(jnp.float32) + full_batch_shift.astype(jnp.float32)
    ).astype(jnp.bfloat16)
    joined = text_rows.astype(jnp.float32) + jnp.einsum(
        "drs,dsc->drc", onehot, embedded, preferred_element_type=jnp.float32
    )
    joined_low = joined.astype(jnp.bfloat16)
    packed = jnp.einsum(
        "drc,ce->dre", joined_low, full_attend, preferred_element_type=jnp.float32
    ).astype(jnp.bfloat16)
    attended, log_total = lax.map(attend_doc, (packed, padding_mask))
    projected = jnp.einsum("drc,ce->dre", attended, full_merge, preferred_element_type=jnp.float32)
    pre_one = joined + projected
    hidden_state = layer_norm(
        pre_one, full_first_gain.astype(jnp.float32), full_first_shift.astype(jnp.float32)
    )
    hidden_reduced_precision = hidden_state.astype(jnp.bfloat16)
    inner_hidden = jnp.einsum(
        "sjq,qy->sjy",
        hidden_reduced_precision,
        gathered_up_weight,
        preferred_element_type=jnp.float32,
    )
    gelu_activated = exact_gelu(inner_hidden).astype(jnp.bfloat16)
    residual_branch = jnp.einsum(
        "zya,av->zyv", gelu_activated, gathered_down_weight, preferred_element_type=jnp.float32
    )
    pre_two = hidden_state + residual_branch
    layer_output = layer_norm(
        pre_two, full_second_gain.astype(jnp.float32), full_second_shift.astype(jnp.float32)
    )
    again = (
        lax.all_gather(visual_matrix, "fsdp", axis=0, tiled=True),
        lax.all_gather(batch_gain, "fsdp", axis=0, tiled=True),
        lax.all_gather(attend_weight, "fsdp", axis=0, tiled=True),
        lax.all_gather(merge_weight, "fsdp", axis=0, tiled=True),
        lax.all_gather(first_gain, "fsdp", axis=0, tiled=True),
        lax.all_gather(up_matrix, "fsdp", axis=0, tiled=True),
        lax.all_gather(down_matrix, "fsdp", axis=0, tiled=True),
        lax.all_gather(second_gain, "fsdp", axis=0, tiled=True),
    )
    (
        visual_pullback,
        back_batch_gain,
        back_attend,
        back_merge,
        back_first_gain,
        up_pullback,
        down_pullback,
        back_second_gain,
    ) = again
    second_back = jax.vjp(
        layer_norm,
        pre_two,
        back_second_gain.astype(jnp.float32),
        full_second_shift.astype(jnp.float32),
    )[1]
    delta_two, second_gain_local, second_shift_local = second_back(cotangent.astype(jnp.float32))
    branch_gradient = delta_two.astype(jnp.bfloat16)
    down_local = jnp.einsum(
        "omt,oms->ts", gelu_activated, branch_gradient, preferred_element_type=jnp.float32
    )
    delta_activated = jnp.einsum(
        "ivj,hj->ivh", branch_gradient, down_pullback, preferred_element_type=jnp.float32
    )
    gelu_back = jax.vjp(exact_gelu, inner_hidden)[1]
    inner_gradient = gelu_back(delta_activated)[0].astype(jnp.bfloat16)
    up_local = jnp.einsum(
        "oih,oiu->hu", hidden_reduced_precision, inner_gradient, preferred_element_type=jnp.float32
    )
    delta_hidden = delta_two + jnp.einsum(
        "wmx,ix->wmi", inner_gradient, up_pullback, preferred_element_type=jnp.float32
    )
    first_back = jax.vjp(
        layer_norm,
        pre_one,
        back_first_gain.astype(jnp.float32),
        full_first_shift.astype(jnp.float32),
    )[1]
    delta_one, first_gain_local, first_shift_local = first_back(delta_hidden)
    delta_projected = delta_one.astype(jnp.bfloat16)
    merge_local = jnp.einsum(
        "drc,dre->ce", attended, delta_projected, preferred_element_type=jnp.float32
    )
    delta_attended = jnp.einsum(
        "dre,ce->drc", delta_projected, back_merge, preferred_element_type=jnp.float32
    ).astype(jnp.bfloat16)
    delta_packed = lax.map(attend_back, (packed, padding_mask, log_total, delta_attended))
    attend_local = jnp.einsum(
        "drc,dre->ce", joined_low, delta_packed, preferred_element_type=jnp.float32
    )
    delta_joined = delta_one + jnp.einsum(
        "dre,ce->drc", delta_packed, back_attend, preferred_element_type=jnp.float32
    )
    delta_embedded = jnp.einsum(
        "drs,drc->dsc",
        onehot_wide,
        delta_joined,
        precision=highest_precision,
        preferred_element_type=jnp.float32,
    )
    shift_total, gain_total = lax.psum(
        (jnp.sum(delta_embedded, axis=(0, 1)), jnp.sum(delta_embedded * normed, axis=(0, 1))),
        ("dp", "fsdp"),
    )
    visual_delta_rows = (
        valid_slot
        * back_batch_gain.astype(jnp.float32)
        * inverse_spread
        * (delta_embedded - shift_total / segment_total - normed * gain_total / segment_total)
    ).astype(jnp.bfloat16)
    visual_local = jnp.einsum(
        "bli,blz->iz", pooled_segments, visual_delta_rows, preferred_element_type=jnp.float32
    )
    delta_pooled = (
        jnp.einsum(
            "zbl,wl->zbw", visual_delta_rows, visual_pullback, preferred_element_type=jnp.float32
        )
        / divisor
    )
    text_gradient = delta_joined + jnp.einsum(
        "drs,dsc->drc",
        onehot_wide,
        delta_pooled,
        precision=highest_precision,
        preferred_element_type=jnp.float32,
    )
    (
        visual_shard,
        attend_shard,
        merge_shard,
        first_gain_shard,
        first_shift_shard,
        up_shard,
        down_shard,
        second_gain_shard,
        second_shift_shard,
    ) = (
        lax.psum_scatter(
            visual_local.astype(jnp.bfloat16), "fsdp", scatter_dimension=0, tiled=True
        ).astype(jnp.float32),
        lax.psum_scatter(
            attend_local.astype(jnp.bfloat16), "fsdp", scatter_dimension=0, tiled=True
        ).astype(jnp.float32),
        lax.psum_scatter(
            merge_local.astype(jnp.bfloat16), "fsdp", scatter_dimension=0, tiled=True
        ).astype(jnp.float32),
        lax.psum_scatter(
            first_gain_local.astype(jnp.bfloat16), "fsdp", scatter_dimension=0, tiled=True
        ).astype(jnp.float32),
        lax.psum_scatter(
            first_shift_local.astype(jnp.bfloat16), "fsdp", scatter_dimension=0, tiled=True
        ).astype(jnp.float32),
        lax.psum_scatter(
            up_local.astype(jnp.bfloat16), "fsdp", scatter_dimension=0, tiled=True
        ).astype(jnp.float32),
        lax.psum_scatter(
            down_local.astype(jnp.bfloat16), "fsdp", scatter_dimension=0, tiled=True
        ).astype(jnp.float32),
        lax.psum_scatter(
            second_gain_local.astype(jnp.bfloat16), "fsdp", scatter_dimension=0, tiled=True
        ).astype(jnp.float32),
        lax.psum_scatter(
            second_shift_local.astype(jnp.bfloat16), "fsdp", scatter_dimension=0, tiled=True
        ).astype(jnp.float32),
    )
    summed = (
        lax.psum(visual_shard.astype(jnp.bfloat16), "dp").astype(jnp.float32),
        lax.psum(attend_shard.astype(jnp.bfloat16), "dp").astype(jnp.float32),
        lax.psum(merge_shard.astype(jnp.bfloat16), "dp").astype(jnp.float32),
        lax.psum(first_gain_shard.astype(jnp.bfloat16), "dp").astype(jnp.float32),
        lax.psum(first_shift_shard.astype(jnp.bfloat16), "dp").astype(jnp.float32),
        lax.psum(up_shard.astype(jnp.bfloat16), "dp").astype(jnp.float32),
        lax.psum(down_shard.astype(jnp.bfloat16), "dp").astype(jnp.float32),
        lax.psum(second_gain_shard.astype(jnp.bfloat16), "dp").astype(jnp.float32),
        lax.psum(second_shift_shard.astype(jnp.bfloat16), "dp").astype(jnp.float32),
    )
    (
        visual_gradient,
        attend_gradient,
        merge_gradient,
        first_gain_gradient,
        first_shift_gradient,
        up_gradient,
        down_gradient,
        second_gain_gradient,
        second_shift_gradient,
    ) = summed
    piece = features // lax.axis_size("fsdp")
    start = lax.axis_index("fsdp") * piece
    batch_gain_gradient = lax.dynamic_slice_in_dim(gain_total, start, piece, 0)
    batch_shift_gradient = lax.dynamic_slice_in_dim(shift_total, start, piece, 0)
    return (
        layer_output,
        text_gradient,
        visual_gradient,
        batch_gain_gradient,
        batch_shift_gradient,
        attend_gradient,
        merge_gradient,
        first_gain_gradient,
        first_shift_gradient,
        up_gradient,
        down_gradient,
        second_gain_gradient,
        second_shift_gradient,
    )


def solution(mesh):
    in_specs = (
        P(("dp", "fsdp"), None, None),
        P("fsdp", None),
        P("fsdp"),
        P("fsdp"),
        P("fsdp", None),
        P("fsdp", None),
        P("fsdp"),
        P("fsdp"),
        P("fsdp", None),
        P("fsdp", None),
        P("fsdp"),
        P("fsdp"),
        P(("dp", "fsdp")),
        P(("dp", "fsdp"), None),
        P(("dp", "fsdp"), None),
        P(("dp", "fsdp"), None, None),
    )
    out_specs = (
        P(("dp", "fsdp"), None, None),
        P(("dp", "fsdp"), None, None),
        P("fsdp", None),
        P("fsdp"),
        P("fsdp"),
        P("fsdp", None),
        P("fsdp", None),
        P("fsdp"),
        P("fsdp"),
        P("fsdp", None),
        P("fsdp", None),
        P("fsdp"),
        P("fsdp"),
    )
    return jax.shard_map(shards, mesh=mesh, in_specs=in_specs, out_specs=out_specs, check_vma=False)
```

profile of v0, /device:TPU:0, one launch (start us, length us, event | category | flops | bytes accessed | tf_op | source)
XLA Modules:
  0.0 913.8 jit_solution(14838720792702939342)
XLA Ops:
  20.4 39.1 %all-reduce.13 = (bf16[768]{0:T(1024)(128)(2,1)S(1)}, bf16[768]{0:T(1024)(128)(2,1)S(1)}, bf16[768]{0:T(1024)(128)(2,1)S(1)}, bf16[768]{0:T(1024)(128)(2,1)S(1)}, bf16[768]{0:T(1024)(128)(2,1)S(1)}) all-reduce(bf16[768]{0:T(1024)(128)(2,1)S(1)} %dynamic-update-slice.1, ...), channel_id=1, replica_groups=mesh['dp'=4,'fsdp'=8] {'fsdp'}, use_global_device_ids=true, to_apply=%add.1 | all-reduce | flops 3840 | bytes 15360
  61.3 2.1 fusion.47
  63.5 2.0 multiply_reduce_fusion.6
  65.5 38.1 %all-reduce.11 = (f32[768]{0:T(1024)S(1)}, f32[]{:T(128)}) all-reduce(f32[768]{0:T(1024)S(1)} %get-tuple-element.172, f32[]{:T(128)S(6)} %convert_element_type.181), channel_id=1, replica_groups=mesh['dp'=4,'fsdp'=8] {'dp','fsdp'}, use_global_device_ids=true, to_apply=%region_2.0 | all-reduce | flops 769 | bytes 6152 | tf_op jit(solution)/shard_map/psum | solution.py:157
  104.5 42.7 %psum.100 = f32[768]{0:T(1024)S(1)} all-reduce(f32[768]{0:T(1024)S(1)} %fusion.53), channel_id=1, replica_groups=mesh['dp'=4,'fsdp'=8] {'dp','fsdp'}, use_global_device_ids=true, to_apply=%region_6.0 | all-reduce | flops 768 | bytes 6144 | tf_op jit(solution)/shard_map/psum | solution.py:163
  147.8 2.3 fusion.55
  150.1 9.0 convolution_convert_fusion
  159.1 6.8 copy.50
  165.9 22.8 %while.22 = (s32[]{:T(128)}, bf16[2,512,768]{1,2,0:T(8,128)(2,1)S(1)}, f32[2,12,512]{2,1,0:T(8,128)S(1)}, bf16[2,512,2304]{1,2,0:T(8,128)(2,1)}, s32[2,512]{1,0:T(2,128)S(1)}, /*index=5*/s32[]{:T(128)}) while((s32[]{:T(128)}, bf16[2,512,768]{1,2,0:T(8,128)(2,1)S(1)}, f32[2,12,512]{2,1,0:T(8,128)S(1)}, bf16[2,512,2304]{1,2,0:T(8,128)(2,1)}, ...), condition=%wide.region_10.11_spmd, body=%wide.region_7.10_spmd.sunk | while | flops 843442688 | bytes 52129876 | solution.py:177
  166.4 1.8 dynamic-slice_bitcast_fusion.6
  168.4 3.1 fusion.131
  171.5 2.6 fusion.132
  174.1 3.3 fusion.133
  177.5 1.8 dynamic-slice_bitcast_fusion.6
  179.5 3.1 fusion.131
  182.6 2.6 fusion.132
  185.2 3.3 fusion.133
  189.9 4.8 fusion.77
  195.2 48.8 %all-gather.12.cloned.1.call-done = bf16[768,3072]{1,0:T(8,128)(2,1)} async-done(((bf16[96,3072]{1,0:T(8,128)(2,1)}), bf16[768,3072]{1,0:T(8,128)(2,1)}) %all-gather.12.cloned.1.call-update) | async-done | bytes 4718608 | tf_op jit(solution)/shard_map/all_gather | solution.py:124
  244.0 14.9 %fusion.36 = (u8[512,3072]{1,0:T(8,128)(4,1)S(1)}, u8[512,3072]{1,0:T(8,128)(4,1)S(1)}, f32[2,512,3072]{2,1,0:T(8,128)}) fusion(bf16[768,3072]{1,0:T(8,128)(2,1)} %all-gather.12.cloned.1.call-done, f32[2,512,768]{2,1,0:T(8,128)S(1)} %get-tuple-element.175, f32[768]{0:T(1024)S(1)} %copy-done.50, f32[768]{0:T(1024)S(1)} %copy-done.40, ...), kind=kOutput, calls=%fused_computation.80 | convolution fusion | flops 4873519104 | bytes 23607296 | tf_op jit(solution)/shard_map/sjq,qy->sjy/dot_general | solution.py:184
  258.9 31.0 %multiply_convert_fusion.3 = (bf16[2,512,3072]{2,1,0:T(8,128)(2,1)}, f32[2,512,3072]{2,1,0:T(8,128)}) fusion(f32[2,512,3072]{2,1,0:T(8,128)} %get-tuple-element.176, u8[512,3072]{1,0:T(8,128)(4,1)S(1)} %get-tuple-element.99, u8[512,3072]{1,0:T(8,128)(4,1)S(1)} %get-tuple-element.98), kind=kLoop, calls=%fused_computation.37 | loop fusion | flops 220200960 | bytes 34603008 | tf_op jit(solution)/shard_map/convert_element_type | solution.py:190
  289.9 34.1 %all-gather.14.cloned.1.call-done = bf16[3072,768]{1,0:T(8,128)(2,1)} async-done(((bf16[384,768]{1,0:T(8,128)(2,1)}), bf16[3072,768]{1,0:T(8,128)(2,1)}) %all-gather.14.cloned.1.call-update) | async-done | bytes 4718608 | tf_op jit(solution)/shard_map/all_gather | solution.py:125
  324.1 9.5 %fusion.78 = (f32[2,512]{1,0:T(2,128)S(1)}, f32[2,512,768]{2,1,0:T(8,128)S(1)}) fusion(bf16[2,512,3072]{2,1,0:T(8,128)(2,1)} %get-tuple-element.156, bf16[3072,768]{1,0:T(8,128)(2,1)} %all-gather.14.cloned.1.call-done, f32[768]{0:T(1024)S(1)} %copy-done.50, f32[768]{0:T(1024)S(1)} %copy-done.40, f32[2,512]{1,0:T(2,128)S(1)} %fusion.66, ...), kind=kOutput, calls=%fused_computation.142 | convolution fusion | flops 4836555776 | bytes 17319936 | tf_op jit(solution)/shard_map/zya,av->zyv/dot_general | solution.py:191
  334.7 2.4 fusion.34
  337.1 16.4 %add_convert_fusion = bf16[2,512,3072]{2,1,0:T(8,128)(2,1)} fusion(f32[2,512,3072]{2,1,0:T(8,128)} %get-tuple-element.157, f32[2,512,3072]{2,1,0:T(8,128)} %get-tuple-element.176, bf16[3072,768]{1,0:T(8,128)(2,1)} %all-gather.14.cloned.1.call-done, f32[2,512]{1,0:T(2,128)S(1)} %negate_multiply_fusion.2, bf16[2,512,768]{2,1,0:T(8,128)(2,1)} %param.35, ...), kind=kOutput, calls=%fused_computation.36 | convolution fusion | flops 4882956288 | bytes 40913920 | tf_op jit(solution)/shard_map/ivj,hj->ivh/dot_general | solution.py:229
  353.5 11.2 %multiply_reduce_fusion.1 = (bf16[768]{0:T(1024)(128)(2,1)}, f32[2,512]{1,0:T(2,128)S(1)}, bf16[768]{0:T(1024)(128)(2,1)}, f32[2,512,768]{2,1,0:T(8,128)S(1)}) fusion(f32[2,512,768]{2,1,0:T(8,128)} %copy-done.2, f32[2,512]{1,0:T(2,128)S(1)} %fusion.66, f32[2,512]{1,0:T(2,128)S(1)} %broadcast_multiply_fusion.1, f32[768]{0:T(1024)S(1)} %copy-done.40, ...), kind=kOutput, calls=%fused_computation.72 | convolution fusion | flops 4845204480 | bytes 22057984 | tf_op jit(solution)/shard_map/wmx,ix->wmi/dot_general | solution.py:237
  366.1 2.5 bitcast_convert_fusion.3
  368.8 3.9 convolution_convert_fusion.1
  372.6 77.6 %while.23 = (s32[]{:T(128)}, bf16[2,512,2304]{1,2,0:T(8,128)(2,1)}, bf16[2,512,2304]{1,2,0:T(8,128)(2,1)}, s32[2,512]{1,0:T(2,128)S(1)}, f32[2,12,512]{2,1,0:T(8...) while((s32[]{:T(128)}, bf16[2,512,2304]{1,2,0:T(8,128)(2,1)}, bf16[2,512,2304]{1,2,0:T(8,128)(2,1)}, ...), condition=%wide.region_21.22_spmd, body=%wide.region_19.21_spmd.sunk | while | flops 2069490176 | bytes 163754704 | solution.py:254
  373.0 1.9 dynamic-slice_bitcast_fusion.7
  375.1 6.4 fusion.145
  383.9 11.5 %multiply_reduce_fusion.8 = (f32[12,512]{1,0:T(8,128)S(1)}, f32[12,512,512]{1,2,0:T(8,128)}) fusion(f32[12,512,512]{1,2,0:T(8,128)} %fusion.145, f32[12,512]{1,0:T(8,128)S(1)} %dynamic-slice_bitcast_fusion.8, pred[512]{0:T(512)(128)(4,1)S(1)} %compare_reduce_fusion.5, bf16[512,12,64]{0,2,1:T(8,128)(2,1)S(1)} %bitcast.169, ...), kind=kOutput, calls=%fused_computation.14.clone.1 | convolution fusion | flops 418375680 | bytes 26788352 | tf_op jit(solution)/shard_map/while/body/eval_jaxpr/qhe,khe->hqk/dot_general | solution.py:67
  396.7 7.1 multiply_convert_fusion.8
  405.0 2.0 multiply_convert_fusion.9
  407.0 3.1 fusion.146
  410.0 1.6 maximum_dynamic-update-slice_fusion.2
  411.6 1.8 dynamic-slice_bitcast_fusion.7
  413.6 6.4 fusion.145
  422.4 11.5 %multiply_reduce_fusion.8 = (f32[12,512]{1,0:T(8,128)S(1)}, f32[12,512,512]{1,2,0:T(8,128)}) fusion(f32[12,512,512]{1,2,0:T(8,128)} %fusion.145, f32[12,512]{1,0:T(8,128)S(1)} %dynamic-slice_bitcast_fusion.8, pred[512]{0:T(512)(128)(4,1)S(1)} %compare_reduce_fusion.5, bf16[512,12,64]{0,2,1:T(8,128)(2,1)S(1)} %bitcast.169, ...), kind=kOutput, calls=%fused_computation.14.clone.1 | convolution fusion | flops 418375680 | bytes 26788352 | tf_op jit(solution)/shard_map/while/body/eval_jaxpr/qhe,khe->hqk/dot_general | solution.py:67
  435.1 7.1 multiply_convert_fusion.8
  443.3 2.0 multiply_convert_fusion.9
  445.3 3.1 fusion.146
  448.4 1.6 maximum_dynamic-update-slice_fusion.2
  450.3 8.5 add_add_fusion.2
  458.8 1.6 copy-done.8
  460.4 1.5 fusion.71
  461.9 38.4 %all-reduce.10 = (f32[768]{0:T(1024)S(1)}, f32[768]{0:T(1024)S(1)}) all-reduce(f32[768]{0:T(1024)S(1)} %get-tuple-element.108, f32[768]{0:T(1024)S(1)} %get-tuple-element.107), channel_id=1, replica_groups=mesh['dp'=4,'fsdp'=8] {'dp','fsdp'}, use_global_device_ids=true, to_apply=%region_25.26 | all-reduce | flops 1536 | bytes 12288 | tf_op jit(solution)/shard_map/psum | solution.py:268
  502.7 1.5 bitcast_convert_fusion.4
  505.0 8.5 bitcast_convert_fusion.2
  513.8 1.6 copy-done.1
  515.4 11.2 %bitcast_convert_fusion = bf16[3072,768]{1,0:T(8,128)(2,1)} fusion(bf16[2,512,3072]{2,1,0:T(8,128)(2,1)} %get-tuple-element.156, f32[2,512]{1,0:T(2,128)S(1)} %copy-done.53, bf16[2,512,768]{2,1,0:T(8,128)(2,1)} %param.35, f32[2,512,768]{2,1,0:T(8,128)S(1)} %copy-done.1, f32[2,512]{1,0:T(2,128)S(1)} %copy-done.46, f32[768]{0:T(1024)S(1)} %copy-done.27, ...), kind=kOutput, calls=%fused_computation.50 | convolution fusion | flops 4841275392 | bytes 15748096 | tf_op jit(solution)/shard_map/omt,oms->ts/dot_general | solution.py:226
  527.3 10.5 %bitcast_convert_fusion.1 = bf16[768,3072]{1,0:T(8,128)(2,1)} fusion(bf16[2,512,3072]{2,1,0:T(8,128)(2,1)} %add_convert_fusion, f32[2,512,768]{2,1,0:T(8,128)} %copy-done.2, f32[768]{0:T(1024)S(1)} %copy-done.51, f32[768]{0:T(1024)S(1)} %copy-done.41, f32[2,512]{1,0:T(2,128)S(1)} %copy-done.43, f32[2,512]{1,0:T(2,128)S(1)} %copy-done.37), kind=kOutput, calls=%fused_computation.51 | convolution fusion | flops 4838129664 | bytes 14170112 | tf_op jit(solution)/shard_map/oih,oiu->hu/dot_general | solution.py:234
  537.9 2.3 reduce_sum.212
  545.3 37.0 %all-reduce.12 = (bf16[768]{0:T(1024)(128)(2,1)}, bf16[768]{0:T(1024)(128)(2,1)}, bf16[768]{0:T(1024)(128)(2,1)}, bf16[768]{0:T(1024)(128)(2,1)}, bf16[768]{0:T(1024)(128)(2,1)}) all-reduce(bf16[768]{0:T(1024)(128)(2,1)} %dynamic-update-slice.5, bf16[768]{0:T(1024)(128)(2,1)} %get-tuple-element.100, ...), channel_id=1, replica_groups=mesh['dp'=4,'fsdp'=8] {'fsdp'}, use_global_device_ids=true, to_apply=%add.5 | all-reduce | flops 3840 | bytes 15360
  587.4 6.9 all-reduce.14
  600.3 50.8 %reduce-scatter.8.cloned.1.call-done = bf16[96,2304]{1,0:T(8,128)(2,1)} async-done(((bf16[768,2304]{1,0:T(8,128)(2,1)}), bf16[96,2304]{1,0:T(8,128)(2,1)}) %reduce-scatter.8.cloned.1.call-update) | async-done | bytes 442384 | tf_op jit(solution)/shard_map/reduce_scatter | solution.py:308
  651.0 98.7 %reduce-scatter.14.cloned.1.call-done = bf16[384,768]{1,0:T(8,128)(2,1)} async-done(((bf16[3072,768]{1,0:T(8,128)(2,1)}), bf16[384,768]{1,0:T(8,128)(2,1)}) %reduce-scatter.14.cloned.1.call-update) | async-done | bytes 589840 | tf_op jit(solution)/shard_map/reduce_scatter | solution.py:323
  749.7 98.5 %reduce-scatter.12.cloned.1.call-done = bf16[96,3072]{1,0:T(8,128)(2,1)} async-done(((bf16[768,3072]{1,0:T(8,128)(2,1)}), bf16[96,3072]{1,0:T(8,128)(2,1)}) %reduce-scatter.12.cloned.1.call-update) | async-done | bytes 589840 | tf_op jit(solution)/shard_map/reduce_scatter | solution.py:320
  848.3 1.8 convolution_divide_fusion
  850.1 2.2 multiply_add_fusion
  853.0 3.2 convolution_add_fusion
  856.2 44.0 %all-reduce.18.cloned.1.call-done = (bf16[96,768]{1,0:T(8,128)(2,1)}, bf16[96,2304]{1,0:T(8,128)(2,1)}, bf16[96,768]{1,0:T(8,128)(2,1)}, bf16[96,3072]{1,0:T(8,128)(2,1)}, bf16[384,768]{1,0:T(8,128)(2,1)}) async-done(((bf16[96,768]{1,0:T(8,128)(2,1)}, bf16[96,2304]{1,0:T(8,128)(2,1)}, bf16[96,768]{1,0:T(8,128)(2,1)}, bf16[96,3072]{1,0:T(8,128)(2,1)}, bf16[384,768]{1,0:T(8,128)(2,1)}), ...) | async-done | bytes 1916944 | tf_op jit(solution)/shard_map/psum | solution.py:334
  900.2 2.2 convert_element_type.210
  902.4 2.2 convert_element_type.212
  (231 shorter events, 52.4 us)
Async XLA Ops:
  7.2 56.3 %all-gather.6.cloned.1.call-start = ((), (), s32[]{:S(2)}) async-start(), calls=%async_computation.5 | async-start | bytes 1327104 | tf_op jit(solution)/shard_map/all_gather | solution.py:117
  7.9 142.2 %all-gather.8.cloned.1.call-start = ((), (), s32[]{:S(2)}) async-start(), calls=%async_computation.6 | async-start | bytes 3981312 | tf_op jit(solution)/shard_map/all_gather | solution.py:120
  8.7 180.1 %all-gather.10.cloned.1.call-start = ((), (), s32[]{:S(2)}) async-start(), calls=%async_computation.7 | async-start | bytes 1327104 | tf_op jit(solution)/shard_map/all_gather | solution.py:121
  9.4 234.6 %all-gather.12.cloned.1.call-start = ((), (), s32[]{:S(2)}) async-start(), calls=%async_computation.8 | async-start | bytes 5308416 | tf_op jit(solution)/shard_map/all_gather | solution.py:124
  10.0 314.1 %all-gather.14.cloned.1.call-start = ((), (), s32[]{:S(2)}) async-start(), calls=%async_computation.9 | async-start | bytes 5308416 | tf_op jit(solution)/shard_map/all_gather | solution.py:125
  10.6 589.7 %reduce-scatter.10.cloned.1.call-start = ((), (), s32[]{:S(2)}) async-start(), calls=%async_computation.12 | async-start | bytes 1327104 | tf_op jit(solution)/shard_map/reduce_scatter | solution.py:311
  11.4 92.9 %copy-start.47 = (f32[2,128]{1,0:T(2,128)}, f32[2,128]{1,0:T(2,128)S(1)}, u32[]{:S(2)}) copy-start(f32[2,128]{1,0:T(2,128)S(1)} %compare_convert_fusion) | copy-start | bytes 3076
  13.6 49.9 %copy-start.57 = (f32[2,128]{1,0:T(2,128)}, f32[2,128]{1,0:T(2,128)S(1)}, u32[]{:S(2)}) copy-start(f32[2,128]{1,0:T(2,128)S(1)} %broadcast_maximum_fusion) | copy-start | bytes 3076
  59.5 88.3 %copy-start.34 = (f32[768]{0:T(1024)}, f32[768]{0:T(1024)S(1)}, u32[]{:S(2)}) copy-start(f32[768]{0:T(1024)S(1)} %convert_element_type.182) | copy-start | bytes 9220
  61.3 86.5 %copy-start.30 = (s32[2,512]{1,0:T(2,128)S(1)}, s32[2,512]{1,0:T(2,128)}, u32[]{:S(2)}) copy-start(s32[2,512]{1,0:T(2,128)} %param.33) | copy-start | bytes 12292
  63.4 86.7 %copy-start.16 = (bf16[2,128,768]{2,1,0:T(8,128)(2,1)}, bf16[2,128,768]{2,1,0:T(8,128)(2,1)S(1)}, u32[]{:S(2)}) copy-start(bf16[2,128,768]{2,1,0:T(8,128)(2,1)S(1)} %fusion.47) | copy-start | bytes 1179652
  63.5 86.7 %copy-start.12 = (bf16[2,512,768]{2,1,0:T(8,128)(2,1)S(1)}, bf16[2,512,768]{2,1,0:T(8,128)(2,1)}, u32[]{:S(2)}) copy-start(bf16[2,512,768]{2,1,0:T(8,128)(2,1)} %param.20) | copy-start | bytes 4718596
  65.5 93.5 %copy-start.4 = (f32[2,128,768]{2,1,0:T(8,128)}, f32[2,128,768]{2,1,0:T(8,128)S(1)}, u32[]{:S(2)}) copy-start(f32[2,128,768]{2,1,0:T(8,128)S(1)} %get-tuple-element.173) | copy-start | bytes 2359300
  104.3 54.8 %copy-start.24 = (f32[768]{0:T(1024)}, f32[768]{0:T(1024)S(1)}, u32[]{:S(2)}) copy-start(f32[768]{0:T(1024)S(1)} %broadcast_divide_fusion.1) | copy-start | bytes 9220
  147.8 11.3 %copy-start.32 = (f32[768]{0:T(1024)}, f32[768]{0:T(1024)S(1)}, u32[]{:S(2)}) copy-start(f32[768]{0:T(1024)S(1)} %add_rsqrt_fusion) | copy-start | bytes 9220
  159.1 6.8 copy-start.13
  159.1 6.8 copy-start.23
  194.6 64.2 %copy-start.2 = (f32[2,512,768]{2,1,0:T(8,128)}, f32[2,512,768]{2,1,0:T(8,128)S(1)}, u32[]{:S(2)}) copy-start(f32[2,512,768]{2,1,0:T(8,128)S(1)} %get-tuple-element.175) | copy-start | bytes 9437188
  194.6 49.3 %copy-start.40 = (f32[768]{0:T(1024)S(1)}, f32[768]{0:T(1024)}, u32[]{:S(2)}) copy-start(f32[768]{0:T(1024)} %convert_element_type.187) | copy-start | bytes 9220
  194.7 49.3 %copy-start.50 = (f32[768]{0:T(1024)S(1)}, f32[768]{0:T(1024)}, u32[]{:S(2)}) copy-start(f32[768]{0:T(1024)} %convert_element_type.188) | copy-start | bytes 9220
  194.7 170.0 %copy-start.36 = (f32[2,512]{1,0:T(2,128)}, f32[2,512]{1,0:T(2,128)S(1)}, u32[]{:S(2)}) copy-start(f32[2,512]{1,0:T(2,128)S(1)} %broadcast_multiply_fusion.1) | copy-start | bytes 12292
  195.2 169.5 %copy-start.42 = (f32[2,512]{1,0:T(2,128)}, f32[2,512]{1,0:T(2,128)S(1)}, u32[]{:S(2)}) copy-start(f32[2,512]{1,0:T(2,128)S(1)} %fusion.66) | copy-start | bytes 12292
  324.1 9.6 %copy-start.6 = (bf16[2,512,768]{2,1,0:T(8,128)(2,1)S(1)}, bf16[2,512,768]{2,1,0:T(8,128)(2,1)}, u32[]{:S(2)}) copy-start(bf16[2,512,768]{2,1,0:T(8,128)(2,1)} %param.35) | copy-start | bytes 4718596
  324.1 9.6 %copy-start.26 = (f32[768]{0:T(1024)S(1)}, f32[768]{0:T(1024)}, u32[]{:S(2)}) copy-start(f32[768]{0:T(1024)} %convert_element_type.191) | copy-start | bytes 9220
  333.6 19.8 %copy-start = (f32[2,512,768]{2,1,0:T(8,128)}, f32[2,512,768]{2,1,0:T(8,128)S(1)}, u32[]{:S(2)}) copy-start(f32[2,512,768]{2,1,0:T(8,128)S(1)} %get-tuple-element.178) | copy-start | bytes 9437188
  333.6 19.8 %copy-start.28 = (f32[2,512]{1,0:T(2,128)}, f32[2,512]{1,0:T(2,128)S(1)}, u32[]{:S(2)}) copy-start(f32[2,512]{1,0:T(2,128)S(1)} %broadcast_multiply_fusion) | copy-start | bytes 12292
  334.7 18.8 %copy-start.38 = (f32[2,512]{1,0:T(2,128)}, f32[2,512]{1,0:T(2,128)S(1)}, u32[]{:S(2)}) copy-start(f32[2,512]{1,0:T(2,128)S(1)} %get-tuple-element.169) | copy-start | bytes 12292
  334.7 18.8 %copy-start.45 = (f32[2,512]{1,0:T(2,128)}, f32[2,512]{1,0:T(2,128)S(1)}, u32[]{:S(2)}) copy-start(f32[2,512]{1,0:T(2,128)S(1)} %get-tuple-element.168) | copy-start | bytes 12292
  337.1 16.4 %copy-start.52 = (f32[2,512]{1,0:T(2,128)}, f32[2,512]{1,0:T(2,128)S(1)}, u32[]{:S(2)}) copy-start(f32[2,512]{1,0:T(2,128)S(1)} %negate_multiply_fusion.2) | copy-start | bytes 12292
  353.5 11.2 %copy-start.3 = (f32[2,512,768]{2,1,0:T(8,128)S(1)}, f32[2,512,768]{2,1,0:T(8,128)}, u32[]{:S(2)}) copy-start(f32[2,512,768]{2,1,0:T(8,128)} %copy-done.2) | copy-start | bytes 9437188
  365.9 2.8 copy-start.11
  366.0 2.8 copy-start.55
  368.7 231.6 %reduce-scatter.6.cloned.1.call-start = ((), (), s32[]{:S(2)}) async-start(), calls=%async_computation.10 | async-start | bytes 1327104 | tf_op jit(solution)/shard_map/reduce_scatter | solution.py:305
  372.6 77.6 %copy-start.56 = (f32[2,512]{1,0:T(2,128)S(1)}, f32[2,512]{1,0:T(2,128)}, u32[]{:S(2)}) copy-start(f32[2,512]{1,0:T(2,128)} %copy-done.55) | copy-start | bytes 12292
  375.1 6.4 copy-start.10
  383.9 11.6 %slice-start = ((s8[12582912]{0:T(1024)(128)(4,1)}), s8[4194304]{0:T(1024)(128)(4,1)S(1)}, s32[]{:S(2)}) async-start(s8[12582912]{0:T(1024)(128)(4,1)} %bitcast.161), calls=%async_computation.16 | async-start | bytes 8388608 | tf_op jit(solution)/shard_map/while
  383.9 11.5 %slice-start.1 = ((s8[12582912]{0:T(1024)(128)(4,1)}), s8[4194304]{0:T(1024)(128)(4,1)S(1)}, s32[]{:S(2)}) async-start(s8[12582912]{0:T(1024)(128)(4,1)} %bitcast.161), calls=%async_computation.17 | async-start | bytes 8388608 | tf_op jit(solution)/shard_map/while
  383.9 12.8 %slice-start.2 = ((s8[12582912]{0:T(1024)(128)(4,1)}), s8[4194304]{0:T(1024)(128)(4,1)S(1)}, s32[]{:S(2)}) async-start(s8[12582912]{0:T(1024)(128)(4,1)} %bitcast.161), calls=%async_computation.18 | async-start | bytes 8388608 | tf_op jit(solution)/shard_map/while
  413.6 6.4 copy-start.10
  422.4 11.5 %slice-start = ((s8[12582912]{0:T(1024)(128)(4,1)}), s8[4194304]{0:T(1024)(128)(4,1)S(1)}, s32[]{:S(2)}) async-start(s8[12582912]{0:T(1024)(128)(4,1)} %bitcast.161), calls=%async_computation.16 | async-start | bytes 8388608 | tf_op jit(solution)/shard_map/while
  422.4 11.5 %slice-start.1 = ((s8[12582912]{0:T(1024)(128)(4,1)}), s8[4194304]{0:T(1024)(128)(4,1)S(1)}, s32[]{:S(2)}) async-start(s8[12582912]{0:T(1024)(128)(4,1)} %bitcast.161), calls=%async_computation.17 | async-start | bytes 8388608 | tf_op jit(solution)/shard_map/while
  422.4 12.7 %slice-start.2 = ((s8[12582912]{0:T(1024)(128)(4,1)}), s8[4194304]{0:T(1024)(128)(4,1)S(1)}, s32[]{:S(2)}) async-start(s8[12582912]{0:T(1024)(128)(4,1)} %bitcast.161), calls=%async_computation.18 | async-start | bytes 8388608 | tf_op jit(solution)/shard_map/while
  450.2 10.2 %copy-start.5 = (f32[2,128,768]{2,1,0:T(8,128)S(1)}, f32[2,128,768]{2,1,0:T(8,128)}, u32[]{:S(2)}) copy-start(f32[2,128,768]{2,1,0:T(8,128)} %copy-done.4) | copy-start | bytes 2359300
  450.2 10.2 %copy-start.25 = (f32[768]{0:T(1024)S(1)}, f32[768]{0:T(1024)}, u32[]{:S(2)}) copy-start(f32[768]{0:T(1024)} %copy-done.24) | copy-start | bytes 9220
  450.2 10.2 %copy-start.31 = (s32[2,512]{1,0:T(2,128)S(1)}, s32[2,512]{1,0:T(2,128)}, u32[]{:S(2)}) copy-start(s32[2,512]{1,0:T(2,128)} %param.33) | copy-start | bytes 12292
  450.2 10.1 %copy-start.33 = (f32[768]{0:T(1024)S(1)}, f32[768]{0:T(1024)}, u32[]{:S(2)}) copy-start(f32[768]{0:T(1024)} %copy-done.32) | copy-start | bytes 9220
  460.4 40.6 %copy-start.35 = (f32[768]{0:T(1024)S(1)}, f32[768]{0:T(1024)}, u32[]{:S(2)}) copy-start(f32[768]{0:T(1024)} %copy-done.34) | copy-start | bytes 9220
  460.4 40.6 %copy-start.48 = (f32[2,128]{1,0:T(2,128)S(1)}, f32[2,128]{1,0:T(2,128)}, u32[]{:S(2)}) copy-start(f32[2,128]{1,0:T(2,128)} %copy-done.47) | copy-start | bytes 3076
  460.4 42.3 %copy-start.17 = (bf16[2,128,768]{2,1,0:T(8,128)(2,1)S(1)}, bf16[2,128,768]{2,1,0:T(8,128)(2,1)}, u32[]{:S(2)}) copy-start(bf16[2,128,768]{2,1,0:T(8,128)(2,1)} %copy-done.16) | copy-start | bytes 1179652
  502.7 2.3 copy-start.7
  504.3 146.8 %reduce-scatter.8.cloned.1.call-start = ((), (), s32[]{:S(2)}) async-start(), calls=%async_computation.11 | async-start | bytes 3981312 | tf_op jit(solution)/shard_map/reduce_scatter | solution.py:308
  513.5 1.9 copy-start.1
  513.5 1.9 copy-start.27
  513.5 1.9 copy-start.29
  513.5 1.9 copy-start.39
  513.5 1.9 copy-start.46
  513.6 236.1 %reduce-scatter.14.cloned.1.call-start = ((), (), s32[]{:S(2)}) async-start(), calls=%async_computation.14 | async-start | bytes 5308416 | tf_op jit(solution)/shard_map/reduce_scatter | solution.py:323
  526.6 321.6 %reduce-scatter.12.cloned.1.call-start = ((), (), s32[]{:S(2)}) async-start(), calls=%async_computation.13 | async-start | bytes 5308416 | tf_op jit(solution)/shard_map/reduce_scatter | solution.py:320
  537.8 310.5 %copy-start.19 = (bf16[2,128,768]{2,1,0:T(8,128)(2,1)S(1)}, bf16[2,128,768]{2,1,0:T(8,128)(2,1)}, u32[]{:S(2)}) copy-start(bf16[2,128,768]{2,1,0:T(8,128)(2,1)} %copy-done.18) | copy-start | bytes 1179652
  537.8 362.3 %all-reduce.18.cloned.1.call-start = ((), (), s32[]{:S(2)}) async-start(), calls=%async_computation.15 | async-start | bytes 3833856 | tf_op jit(solution)/shard_map/psum | solution.py:334
  850.1 2.9 copy-start.9
  900.2 4.4 copy-start.20
  900.2 5.4 copy-start.22
  900.2 6.1 copy-start.21
  (12 other events, 12.7 us)
Sparse Core Ops, SparseCore 0:
  10.2 44.0 all-gather.5
  56.5 64.8 all-gather.7
  123.5 39.6 all-gather.9
  165.3 78.6 all-gather.11
  246.0 78.0 all-gather.13
  368.8 62.2 reduce-scatter.9
  504.4 64.7 reduce-scatter.5
  572.9 78.1 reduce-scatter.7
  654.7 94.9 reduce-scatter.13
  753.2 95.0 reduce-scatter.11
  851.0 49.1 all-reduce.17
where the time goes:
time: 922 us; the launch traced here: 914 us
  waiting for transfers between devices  378 us (41%)
  blocking collectives  202 us (22%)
  matrix products  186 us (20%)
  other arithmetic  84 us (9%)
  local copies, waits for them, and re-layouts  44.5 us (5%)
  between operations  16.8 us (2%)
    reduce_scatter x1, waiting for transfers between devices, shards(): lax.psum_scatter(down_local.astype(jnp.bfloat16), 'fsdp', scatter_dimensi...  98.7 us
    reduce_scatter x1, waiting for transfers between devices, shards(): lax.psum_scatter(up_local.astype(jnp.bfloat16), 'fsdp', scatter_dimension...  98.5 us
    unnamed x2, blocking collectives  76.1 us
    reduce_scatter x1, waiting for transfers between devices, shards(): lax.psum_scatter(attend_local.astype(jnp.bfloat16), 'fsdp', scatter_dimen...  50.8 us
    all_gather x1, waiting for transfers between devices, shards(): lax.all_gather(up_matrix, 'fsdp', axis=0, tiled=True)  48.8 us
    psum x1, waiting for transfers between devices, shards(): lax.psum(visual_shard.astype(jnp.bfloat16), 'dp').astype(jnp.float32)  44 us
    psum x1, blocking collectives, shards(): lax.psum(jnp.sum(valid_slot * center * center, axis=(0, 1)), ('dp', 'fsdp'))  42.7 us
    psum x1, blocking collectives, shards(): lax.psum((jnp.sum(delta_embedded, axis=(0, 1)), jnp.sum(delta_embedded *...  38.4 us
  transfers between devices with their start and end apart: 11, of which 6 were waited for; matrix products, arithmetic and copies ran while one was open for 28% of the time, Pallas kernels for 0%

commit v1 on v0

--- a/solution.py
+++ b/solution.py
@@ -9,6 +9,10 @@
 eps_batch = 1e-05
 masked_score = -1e30
 highest_precision = lax.Precision.HIGHEST
+
+
+def expand_strips_all(block_here, a_name):
+    return jnp.sum(jax.lax.all_gather(block_here, a_name), axis=0)
 
 
 def layer_norm(values, gain, shift):
@@ -331,7 +335,7 @@
         ).astype(jnp.float32),
     )
     summed = (
-        lax.psum(visual_shard.astype(jnp.bfloat16), "dp").astype(jnp.float32),
+        expand_strips_all(visual_shard.astype(jnp.bfloat16), "dp").astype(jnp.float32),
         lax.psum(attend_shard.astype(jnp.bfloat16), "dp").astype(jnp.float32),
         lax.psum(merge_shard.astype(jnp.bfloat16), "dp").astype(jnp.float32),
         lax.psum(first_gain_shard.astype(jnp.bfloat16), "dp").astype(jnp.float32),

time: 922 us -> 872 us (0.946)
  waiting for transfers between devices: 378 us -> 326 us
  blocking collectives: 202 us -> 212 us
    reduce_scatter x1, waiting for transfers between devices: 0.01 us -> 62.7 us  [shards(): lax.psum_scatter(visual_local.astype(jnp.bfloat16), 'fsdp', scatter_dimen...]
    reduce_scatter x1, waiting for transfers between devices: 98.7 us -> 39 us  [shards(): lax.psum_scatter(down_local.astype(jnp.bfloat16), 'fsdp', scatter_dimensi...]
    reduce_scatter x1, waiting for transfers between devices: 50.8 us -> 0.01 us  [shards(): lax.psum_scatter(attend_local.astype(jnp.bfloat16), 'fsdp', scatter_dimen...]
    unnamed x131 -> x119, local copies, waits for them, and re-layouts: 19.9 us -> 11.9 us
  transfers between devices with their start and end apart: 11 -> 11, of which waited for: 6 -> 6; matrix products, arithmetic and copies ran while one was open for 28% -> 29% of each run, Pallas kernels for 0% -> 0%
where the time goes in v1:
time: 872 us; the launch traced here: 864 us
  waiting for transfers between devices  326 us (37%)
  blocking collectives  212 us (24%)
  matrix products  189 us (22%)
  other arithmetic  81.6 us (9%)
  local copies, waits for them, and re-layouts  36.6 us (4%)
  between operations  16.8 us (2%)
    reduce_scatter x1, waiting for transfers between devices, shards(): lax.psum_scatter(up_local.astype(jnp.bfloat16), 'fsdp', scatter_dimension...  98.8 us
    unnamed x2, blocking collectives  78.2 us
    reduce_scatter x1, waiting for transfers between devices, shards(): lax.psum_scatter(visual_local.astype(jnp.bfloat16), 'fsdp', scatter_dimen...  62.7 us
    all_gather x1, waiting for transfers between devices, shards(): lax.all_gather(up_matrix, 'fsdp', axis=0, tiled=True)  48.8 us
    psum x1, blocking collectives, shards(): lax.psum(jnp.sum(valid_slot * center * center, axis=(0, 1)), ('dp', 'fsdp'))  42.7 us
    psum x1, waiting for transfers between devices, shards(): lax.psum(attend_shard.astype(jnp.bfloat16), 'dp').astype(jnp.float32)  39.7 us
    psum x1, blocking collectives, shards(): lax.psum((jnp.sum(delta_embedded, axis=(0, 1)), jnp.sum(delta_embedded *...  39.3 us
    reduce_scatter x1, waiting for transfers between devices, shards(): lax.psum_scatter(down_local.astype(jnp.bfloat16), 'fsdp', scatter_dimensi...  39 us
  transfers between devices with their start and end apart: 11, of which 6 were waited for; matrix products, arithmetic and copies ran while one was open for 29% of the time, Pallas kernels for 0%

profile of v1, /device:TPU:0, one launch (start us, length us, event | category | flops | bytes accessed | tf_op | source)
XLA Modules:
  0.0 864.1 jit_solution(16278802420608402457)
XLA Ops:
  20.4 39.1 %all-reduce.13 = (bf16[768]{0:T(1024)(128)(2,1)S(1)}, bf16[768]{0:T(1024)(128)(2,1)S(1)}, bf16[768]{0:T(1024)(128)(2,1)S(1)}, bf16[768]{0:T(1024)(128)(2,1)S(1)}, bf16[768]{0:T(1024)(128)(2,1)S(1)}) all-reduce(bf16[768]{0:T(1024)(128)(2,1)S(1)} %dynamic-update-slice.1, ...), channel_id=1, replica_groups=mesh['dp'=4,'fsdp'=8] {'fsdp'}, use_global_device_ids=true, to_apply=%add.1 | all-reduce | flops 3840 | bytes 15360
  61.3 2.1 fusion.47
  63.5 2.0 multiply_reduce_fusion.6
  65.6 38.1 %all-reduce.11 = (f32[768]{0:T(1024)S(1)}, f32[]{:T(128)}) all-reduce(f32[768]{0:T(1024)S(1)} %get-tuple-element.171, f32[]{:T(128)S(6)} %convert_element_type.183), channel_id=1, replica_groups=mesh['dp'=4,'fsdp'=8] {'dp','fsdp'}, use_global_device_ids=true, to_apply=%region_2.0 | all-reduce | flops 769 | bytes 6152 | tf_op jit(solution)/shard_map/psum | solution.py:161
  104.5 42.7 %psum.93 = f32[768]{0:T(1024)S(1)} all-reduce(f32[768]{0:T(1024)S(1)} %fusion.53), channel_id=1, replica_groups=mesh['dp'=4,'fsdp'=8] {'dp','fsdp'}, use_global_device_ids=true, to_apply=%region_6.0 | all-reduce | flops 768 | bytes 6144 | tf_op jit(solution)/shard_map/psum | solution.py:167
  147.8 2.3 fusion.55
  150.1 8.9 %convolution_convert_fusion = bf16[2,512,2304]{2,1,0:T(8,128)(2,1)} fusion(bf16[768,2304]{1,0:T(8,128)(2,1)} %all-gather.9.cloned.1.call-done, f32[2,512,768]{2,1,0:T(8,128)} %fusion.55, bf16[2,512,768]{2,1,0:T(8,128)(2,1)S(1)} %copy-done.11), kind=kOutput, calls=%fused_computation.53 | convolution fusion | flops 3628597248 | bytes 12976128 | tf_op jit(solution)/shard_map/drc,ce->dre/dot_general | solution.py:178
  159.1 6.8 copy.50
  165.9 22.8 %while.22 = (s32[]{:T(128)}, bf16[2,512,768]{1,2,0:T(8,128)(2,1)S(1)}, f32[2,12,512]{2,1,0:T(8,128)S(1)}, bf16[2,512,2304]{1,2,0:T(8,128)(2,1)}, s32[2,512]{1,0:T(2,128)S(1)}, /*index=5*/s32[]{:T(128)}) while((s32[]{:T(128)}, bf16[2,512,768]{1,2,0:T(8,128)(2,1)S(1)}, f32[2,12,512]{2,1,0:T(8,128)S(1)}, bf16[2,512,2304]{1,2,0:T(8,128)(2,1)}, ...), condition=%wide.region_10.11_spmd, body=%wide.region_7.10_spmd.sunk | while | flops 843442688 | bytes 52129876 | solution.py:181
  166.4 1.8 dynamic-slice_bitcast_fusion.6
  168.4 3.1 fusion.131
  171.5 2.6 fusion.132
  174.1 3.3 fusion.133
  177.5 1.8 dynamic-slice_bitcast_fusion.6
  179.5 3.1 fusion.131
  182.6 2.6 fusion.132
  185.2 3.3 fusion.133
  189.9 4.8 fusion.77
  195.2 48.8 %all-gather.13.cloned.1.call-done = bf16[768,3072]{1,0:T(8,128)(2,1)} async-done(((bf16[96,3072]{1,0:T(8,128)(2,1)}), bf16[768,3072]{1,0:T(8,128)(2,1)}) %all-gather.13.cloned.1.call-update) | async-done | bytes 4718608 | tf_op jit(solution)/shard_map/all_gather | solution.py:128
  244.0 14.9 %fusion.36 = (u8[512,3072]{1,0:T(8,128)(4,1)S(1)}, u8[512,3072]{1,0:T(8,128)(4,1)S(1)}, f32[2,512,3072]{2,1,0:T(8,128)}) fusion(bf16[768,3072]{1,0:T(8,128)(2,1)} %all-gather.13.cloned.1.call-done, f32[2,512,768]{2,1,0:T(8,128)S(1)} %get-tuple-element.174, f32[768]{0:T(1024)S(1)} %copy-done.45, f32[768]{0:T(1024)S(1)} %copy-done.38, ...), kind=kOutput, calls=%fused_computation.80 | convolution fusion | flops 4873519104 | bytes 23607296 | tf_op jit(solution)/shard_map/sjq,qy->sjy/dot_general | solution.py:188
  258.9 31.0 %multiply_convert_fusion.3 = (bf16[2,512,3072]{2,1,0:T(8,128)(2,1)}, f32[2,512,3072]{2,1,0:T(8,128)}) fusion(f32[2,512,3072]{2,1,0:T(8,128)} %get-tuple-element.175, u8[512,3072]{1,0:T(8,128)(4,1)S(1)} %get-tuple-element.99, u8[512,3072]{1,0:T(8,128)(4,1)S(1)} %get-tuple-element.98), kind=kLoop, calls=%fused_computation.37 | loop fusion | flops 220200960 | bytes 34603008 | tf_op jit(solution)/shard_map/convert_element_type | solution.py:194
  289.9 34.1 %all-gather.15.cloned.1.call-done = bf16[3072,768]{1,0:T(8,128)(2,1)} async-done(((bf16[384,768]{1,0:T(8,128)(2,1)}), bf16[3072,768]{1,0:T(8,128)(2,1)}) %all-gather.15.cloned.1.call-update) | async-done | bytes 4718608 | tf_op jit(solution)/shard_map/all_gather | solution.py:129
  324.1 9.5 %fusion.78 = (f32[2,512]{1,0:T(2,128)S(1)}, f32[2,512,768]{2,1,0:T(8,128)S(1)}) fusion(bf16[2,512,3072]{2,1,0:T(8,128)(2,1)} %get-tuple-element.155, bf16[3072,768]{1,0:T(8,128)(2,1)} %all-gather.15.cloned.1.call-done, f32[768]{0:T(1024)S(1)} %copy-done.45, f32[768]{0:T(1024)S(1)} %copy-done.38, f32[2,512]{1,0:T(2,128)S(1)} %fusion.66, ...), kind=kOutput, calls=%fused_computation.142 | convolution fusion | flops 4836555776 | bytes 17319936 | tf_op jit(solution)/shard_map/zya,av->zyv/dot_general | solution.py:195
  334.7 2.4 fusion.34
  337.1 16.4 %add_convert_fusion = bf16[2,512,3072]{2,1,0:T(8,128)(2,1)} fusion(f32[2,512,3072]{2,1,0:T(8,128)} %get-tuple-element.156, f32[2,512,3072]{2,1,0:T(8,128)} %get-tuple-element.175, bf16[3072,768]{1,0:T(8,128)(2,1)} %all-gather.15.cloned.1.call-done, f32[2,512]{1,0:T(2,128)S(1)} %negate_multiply_fusion.2, bf16[2,512,768]{2,1,0:T(8,128)(2,1)} %param.35, ...), kind=kOutput, calls=%fused_computation.36 | convolution fusion | flops 4882956288 | bytes 40913920 | tf_op jit(solution)/shard_map/ivj,hj->ivh/dot_general | solution.py:233
  353.5 11.2 %multiply_reduce_fusion.1 = (bf16[768]{0:T(1024)(128)(2,1)}, f32[2,512]{1,0:T(2,128)S(1)}, bf16[768]{0:T(1024)(128)(2,1)}, f32[2,512,768]{2,1,0:T(8,128)S(1)}) fusion(f32[2,512,768]{2,1,0:T(8,128)} %copy-done.2, f32[2,512]{1,0:T(2,128)S(1)} %fusion.66, f32[2,512]{1,0:T(2,128)S(1)} %broadcast_multiply_fusion.1, f32[768]{0:T(1024)S(1)} %copy-done.38, ...), kind=kOutput, calls=%fused_computation.72 | convolution fusion | flops 4845204480 | bytes 22057984 | tf_op jit(solution)/shard_map/wmx,ix->wmi/dot_general | solution.py:241
  366.2 2.5 bitcast_convert_fusion.3
  368.8 3.9 convolution_convert_fusion.1
  372.7 77.6 %while.23 = (s32[]{:T(128)}, bf16[2,512,2304]{1,2,0:T(8,128)(2,1)}, bf16[2,512,2304]{1,2,0:T(8,128)(2,1)}, s32[2,512]{1,0:T(2,128)S(1)}, f32[2,12,512]{2,1,0:T(8...) while((s32[]{:T(128)}, bf16[2,512,2304]{1,2,0:T(8,128)(2,1)}, bf16[2,512,2304]{1,2,0:T(8,128)(2,1)}, ...), condition=%wide.region_21.22_spmd, body=%wide.region_19.21_spmd.sunk | while | flops 2069490176 | bytes 163754704 | solution.py:258
  373.1 1.9 dynamic-slice_bitcast_fusion.7
  375.2 6.4 fusion.145
  384.0 11.5 %multiply_reduce_fusion.8 = (f32[12,512]{1,0:T(8,128)S(1)}, f32[12,512,512]{1,2,0:T(8,128)}) fusion(f32[12,512,512]{1,2,0:T(8,128)} %fusion.145, f32[12,512]{1,0:T(8,128)S(1)} %dynamic-slice_bitcast_fusion.8, pred[512]{0:T(512)(128)(4,1)S(1)} %compare_reduce_fusion.5, bf16[512,12,64]{0,2,1:T(8,128)(2,1)S(1)} %bitcast.170, ...), kind=kOutput, calls=%fused_computation.14.clone.1 | convolution fusion | flops 418375680 | bytes 26788352 | tf_op jit(solution)/shard_map/while/body/eval_jaxpr/qhe,khe->hqk/dot_general | solution.py:71
  396.8 7.1 multiply_convert_fusion.8
  405.1 2.0 multiply_convert_fusion.9
  407.1 3.1 fusion.146
  410.2 1.6 maximum_dynamic-update-slice_fusion.2
  411.8 1.8 dynamic-slice_bitcast_fusion.7
  413.8 6.4 fusion.145
  422.6 11.5 %multiply_reduce_fusion.8 = (f32[12,512]{1,0:T(8,128)S(1)}, f32[12,512,512]{1,2,0:T(8,128)}) fusion(f32[12,512,512]{1,2,0:T(8,128)} %fusion.145, f32[12,512]{1,0:T(8,128)S(1)} %dynamic-slice_bitcast_fusion.8, pred[512]{0:T(512)(128)(4,1)S(1)} %compare_reduce_fusion.5, bf16[512,12,64]{0,2,1:T(8,128)(2,1)S(1)} %bitcast.170, ...), kind=kOutput, calls=%fused_computation.14.clone.1 | convolution fusion | flops 418375680 | bytes 26788352 | tf_op jit(solution)/shard_map/while/body/eval_jaxpr/qhe,khe->hqk/dot_general | solution.py:71
  435.3 7.1 multiply_convert_fusion.8
  443.5 2.0 multiply_convert_fusion.9
  445.5 3.1 fusion.146
  448.6 1.6 maximum_dynamic-update-slice_fusion.2
  450.4 9.4 %bitcast_convert_fusion.2 = bf16[768,2304]{1,0:T(8,128)(2,1)} fusion(bf16[2,512,2304]{1,2,0:T(8,128)(2,1)} %get-tuple-element.75, f32[2,512,768]{2,1,0:T(8,128)} %fusion.55, bf16[2,512,768]{2,1,0:T(8,128)(2,1)} %param.20), kind=kOutput, calls=%fused_computation.52 | convolution fusion | flops 3628007424 | bytes 12976128 | tf_op jit(solution)/shard_map/drc,dre->ce/dot_general | solution.py:259
  459.9 1.8 copy-done.1
  461.7 11.2 %bitcast_convert_fusion = bf16[3072,768]{1,0:T(8,128)(2,1)} fusion(bf16[2,512,3072]{2,1,0:T(8,128)(2,1)} %get-tuple-element.155, f32[2,512]{1,0:T(2,128)S(1)} %copy-done.50, bf16[2,512,768]{2,1,0:T(8,128)(2,1)} %param.35, f32[2,512,768]{2,1,0:T(8,128)S(1)} %copy-done.1, f32[2,512]{1,0:T(2,128)S(1)} %copy-done.43, f32[768]{0:T(1024)S(1)} %copy-done.25, ...), kind=kOutput, calls=%fused_computation.50 | convolution fusion | flops 4841275392 | bytes 15748096 | tf_op jit(solution)/shard_map/omt,oms->ts/dot_general | solution.py:230
  473.6 10.7 %bitcast_convert_fusion.1 = bf16[768,3072]{1,0:T(8,128)(2,1)} fusion(bf16[2,512,3072]{2,1,0:T(8,128)(2,1)} %add_convert_fusion, f32[2,512,768]{2,1,0:T(8,128)} %copy-done.2, f32[768]{0:T(1024)S(1)} %copy-done.46, f32[768]{0:T(1024)S(1)} %copy-done.39, f32[2,512]{1,0:T(2,128)S(1)} %copy-done.41, f32[2,512]{1,0:T(2,128)S(1)} %copy-done.34), kind=kOutput, calls=%fused_computation.51 | convolution fusion | flops 4838129664 | bytes 14170112 | tf_op jit(solution)/shard_map/oih,oiu->hu/dot_general | solution.py:238
  484.9 8.6 add_add_fusion.2
  493.6 3.0 fusion.71
  496.6 39.3 %all-reduce.10 = (f32[768]{0:T(1024)}, f32[768]{0:T(1024)}) all-reduce(f32[768]{0:T(1024)} %get-tuple-element.108, f32[768]{0:T(1024)} %get-tuple-element.107), channel_id=1, replica_groups=mesh['dp'=4,'fsdp'=8] {'dp','fsdp'}, use_global_device_ids=true, to_apply=%region_25.26 | all-reduce | flops 1536 | bytes 12288 | tf_op jit(solution)/shard_map/psum | solution.py:272
  537.2 2.3 multiply_convert_fusion.4
  541.8 1.7 reduce_sum.227
  547.6 39.1 %all-reduce.12 = (bf16[768]{0:T(1024)(128)(2,1)S(1)}, bf16[768]{0:T(1024)(128)(2,1)S(1)}, bf16[768]{0:T(1024)(128)(2,1)S(1)}, bf16[768]{0:T(1024)(128)(2,1)S(1)}, bf16[768]{0:T(1024)(128)(2,1)S(1)}) all-reduce(bf16[768]{0:T(1024)(128)(2,1)S(1)} %dynamic-update-slice.5, ...), channel_id=1, replica_groups=mesh['dp'=4,'fsdp'=8] {'fsdp'}, use_global_device_ids=true, to_apply=%add.5 | all-reduce | flops 3840 | bytes 15360
  587.0 6.3 all-reduce.14
  595.4 2.2 multiply_add_fusion
  597.6 39.0 %reduce-scatter.14.cloned.1.call-done = bf16[384,768]{1,0:T(8,128)(2,1)} async-done(((bf16[3072,768]{1,0:T(8,128)(2,1)}), bf16[384,768]{1,0:T(8,128)(2,1)}) %reduce-scatter.14.cloned.1.call-update) | async-done | bytes 589840 | tf_op jit(solution)/shard_map/reduce_scatter | solution.py:327
  636.5 98.8 %reduce-scatter.12.cloned.1.call-done = bf16[96,3072]{1,0:T(8,128)(2,1)} async-done(((bf16[768,3072]{1,0:T(8,128)(2,1)}), bf16[96,3072]{1,0:T(8,128)(2,1)}) %reduce-scatter.12.cloned.1.call-update) | async-done | bytes 589840 | tf_op jit(solution)/shard_map/reduce_scatter | solution.py:324
  735.4 1.8 convolution_divide_fusion
  737.2 3.1 convolution_add_fusion
  740.3 62.7 %reduce-scatter.6.cloned.1.call-done = bf16[96,768]{1,0:T(8,128)(2,1)} async-done(((bf16[768,768]{1,0:T(8,128)(2,1)}), bf16[96,768]{1,0:T(8,128)(2,1)}) %reduce-scatter.6.cloned.1.call-update) | async-done | bytes 147472 | tf_op jit(solution)/shard_map/reduce_scatter | solution.py:309
  803.0 7.7 all-gather
  811.5 39.7 %all-reduce.18.cloned.1.call-done = (bf16[96,2304]{1,0:T(8,128)(2,1)}, bf16[96,768]{1,0:T(8,128)(2,1)}, bf16[96,3072]{1,0:T(8,128)(2,1)}, bf16[384,768]{1,0:T(8,128)(2,1)}) async-done(((bf16[96,2304]{1,0:T(8,128)(2,1)}, bf16[96,768]{1,0:T(8,128)(2,1)}, bf16[96,3072]{1,0:T(8,128)(2,1)}, bf16[384,768]{1,0:T(8,128)(2,1)}), (bf16[96,2304]{1,0:T(8,128)(2,1)}, bf16[96,768]{1,0:T(8,128)(2,1)}, ...) | async-done | bytes 1769488 | tf_op jit(solution)/shard_map/psum | solution.py:339
  851.2 2.2 convert_element_type.212
  853.5 2.2 convert_element_type.214
  (221 shorter events, 43.1 us)
Async XLA Ops:
  7.2 56.3 %all-gather.7.cloned.1.call-start = ((), (), s32[]{:S(2)}) async-start(), calls=%async_computation.5 | async-start | bytes 1327104 | tf_op jit(solution)/shard_map/all_gather | solution.py:121
  7.9 142.2 %all-gather.9.cloned.1.call-start = ((), (), s32[]{:S(2)}) async-start(), calls=%async_computation.6 | async-start | bytes 3981312 | tf_op jit(solution)/shard_map/all_gather | solution.py:124
  8.7 180.1 %all-gather.11.cloned.1.call-start = ((), (), s32[]{:S(2)}) async-start(), calls=%async_computation.7 | async-start | bytes 1327104 | tf_op jit(solution)/shard_map/all_gather | solution.py:125
  9.4 234.6 %all-gather.13.cloned.1.call-start = ((), (), s32[]{:S(2)}) async-start(), calls=%async_computation.8 | async-start | bytes 5308416 | tf_op jit(solution)/shard_map/all_gather | solution.py:128
  10.0 314.1 %all-gather.15.cloned.1.call-start = ((), (), s32[]{:S(2)}) async-start(), calls=%async_computation.9 | async-start | bytes 5308416 | tf_op jit(solution)/shard_map/all_gather | solution.py:129
  10.6 587.0 %reduce-scatter.10.cloned.1.call-start = ((), (), s32[]{:S(2)}) async-start(), calls=%async_computation.12 | async-start | bytes 1327104 | tf_op jit(solution)/shard_map/reduce_scatter | solution.py:315
  11.4 92.9 %copy-start.44 = (f32[2,128]{1,0:T(2,128)}, f32[2,128]{1,0:T(2,128)S(1)}, u32[]{:S(2)}) copy-start(f32[2,128]{1,0:T(2,128)S(1)} %compare_convert_fusion) | copy-start | bytes 3076
  13.6 49.9 %copy-start.51 = (f32[2,128]{1,0:T(2,128)}, f32[2,128]{1,0:T(2,128)S(1)}, u32[]{:S(2)}) copy-start(f32[2,128]{1,0:T(2,128)S(1)} %broadcast_maximum_fusion) | copy-start | bytes 3076
  59.5 88.3 %copy-start.32 = (f32[768]{0:T(1024)}, f32[768]{0:T(1024)S(1)}, u32[]{:S(2)}) copy-start(f32[768]{0:T(1024)S(1)} %convert_element_type.184) | copy-start | bytes 9220
  61.3 86.5 %copy-start.28 = (s32[2,512]{1,0:T(2,128)S(1)}, s32[2,512]{1,0:T(2,128)}, u32[]{:S(2)}) copy-start(s32[2,512]{1,0:T(2,128)} %param.33) | copy-start | bytes 12292
  63.4 86.7 %copy-start.15 = (bf16[2,128,768]{2,1,0:T(8,128)(2,1)}, bf16[2,128,768]{2,1,0:T(8,128)(2,1)S(1)}, u32[]{:S(2)}) copy-start(bf16[2,128,768]{2,1,0:T(8,128)(2,1)S(1)} %fusion.47) | copy-start | bytes 1179652
  63.5 86.7 %copy-start.11 = (bf16[2,512,768]{2,1,0:T(8,128)(2,1)S(1)}, bf16[2,512,768]{2,1,0:T(8,128)(2,1)}, u32[]{:S(2)}) copy-start(bf16[2,512,768]{2,1,0:T(8,128)(2,1)} %param.20) | copy-start | bytes 4718596
  65.5 93.5 %copy-start.4 = (f32[2,128,768]{2,1,0:T(8,128)}, f32[2,128,768]{2,1,0:T(8,128)S(1)}, u32[]{:S(2)}) copy-start(f32[2,128,768]{2,1,0:T(8,128)S(1)} %get-tuple-element.172) | copy-start | bytes 2359300
  104.3 54.8 %copy-start.22 = (f32[768]{0:T(1024)}, f32[768]{0:T(1024)S(1)}, u32[]{:S(2)}) copy-start(f32[768]{0:T(1024)S(1)} %broadcast_divide_fusion.1) | copy-start | bytes 9220
  147.8 11.2 %copy-start.30 = (f32[768]{0:T(1024)}, f32[768]{0:T(1024)S(1)}, u32[]{:S(2)}) copy-start(f32[768]{0:T(1024)S(1)} %add_rsqrt_fusion) | copy-start | bytes 9220
  159.1 6.8 copy-start.12
  159.1 6.8 copy-start.21
  188.7 1.2 copy-start.13
  194.6 64.2 %copy-start.2 = (f32[2,512,768]{2,1,0:T(8,128)}, f32[2,512,768]{2,1,0:T(8,128)S(1)}, u32[]{:S(2)}) copy-start(f32[2,512,768]{2,1,0:T(8,128)S(1)} %get-tuple-element.174) | copy-start | bytes 9437188
  194.6 49.3 %copy-start.38 = (f32[768]{0:T(1024)S(1)}, f32[768]{0:T(1024)}, u32[]{:S(2)}) copy-start(f32[768]{0:T(1024)} %convert_element_type.189) | copy-start | bytes 9220
  194.6 49.3 %copy-start.45 = (f32[768]{0:T(1024)S(1)}, f32[768]{0:T(1024)}, u32[]{:S(2)}) copy-start(f32[768]{0:T(1024)} %convert_element_type.190) | copy-start | bytes 9220
  194.7 170.1 %copy-start.33 = (f32[2,512]{1,0:T(2,128)}, f32[2,512]{1,0:T(2,128)S(1)}, u32[]{:S(2)}) copy-start(f32[2,512]{1,0:T(2,128)S(1)} %broadcast_multiply_fusion.1) | copy-start | bytes 12292
  195.2 169.6 %copy-start.40 = (f32[2,512]{1,0:T(2,128)}, f32[2,512]{1,0:T(2,128)S(1)}, u32[]{:S(2)}) copy-start(f32[2,512]{1,0:T(2,128)S(1)} %fusion.66) | copy-start | bytes 12292
  324.1 9.6 %copy-start.6 = (bf16[2,512,768]{2,1,0:T(8,128)(2,1)S(1)}, bf16[2,512,768]{2,1,0:T(8,128)(2,1)}, u32[]{:S(2)}) copy-start(bf16[2,512,768]{2,1,0:T(8,128)(2,1)} %param.35) | copy-start | bytes 4718596
  324.1 9.6 %copy-start.24 = (f32[768]{0:T(1024)S(1)}, f32[768]{0:T(1024)}, u32[]{:S(2)}) copy-start(f32[768]{0:T(1024)} %convert_element_type.193) | copy-start | bytes 9220
  333.6 19.9 %copy-start = (f32[2,512,768]{2,1,0:T(8,128)}, f32[2,512,768]{2,1,0:T(8,128)S(1)}, u32[]{:S(2)}) copy-start(f32[2,512,768]{2,1,0:T(8,128)S(1)} %get-tuple-element.177) | copy-start | bytes 9437188
  333.6 19.8 %copy-start.26 = (f32[2,512]{1,0:T(2,128)}, f32[2,512]{1,0:T(2,128)S(1)}, u32[]{:S(2)}) copy-start(f32[2,512]{1,0:T(2,128)S(1)} %broadcast_multiply_fusion) | copy-start | bytes 12292
  334.7 18.8 %copy-start.35 = (f32[2,512]{1,0:T(2,128)}, f32[2,512]{1,0:T(2,128)S(1)}, u32[]{:S(2)}) copy-start(f32[2,512]{1,0:T(2,128)S(1)} %get-tuple-element.168) | copy-start | bytes 12292
  334.7 18.8 %copy-start.42 = (f32[2,512]{1,0:T(2,128)}, f32[2,512]{1,0:T(2,128)S(1)}, u32[]{:S(2)}) copy-start(f32[2,512]{1,0:T(2,128)S(1)} %get-tuple-element.167) | copy-start | bytes 12292
  337.1 16.4 %copy-start.49 = (f32[2,512]{1,0:T(2,128)}, f32[2,512]{1,0:T(2,128)S(1)}, u32[]{:S(2)}) copy-start(f32[2,512]{1,0:T(2,128)S(1)} %negate_multiply_fusion.2) | copy-start | bytes 12292
  353.5 11.3 %copy-start.3 = (f32[2,512,768]{2,1,0:T(8,128)S(1)}, f32[2,512,768]{2,1,0:T(8,128)}, u32[]{:S(2)}) copy-start(f32[2,512,768]{2,1,0:T(8,128)} %copy-done.2) | copy-start | bytes 9437188
  364.8 1.4 copy-start.14
  366.0 2.8 copy-start.10
  366.0 2.8 copy-start.47
  368.7 228.8 %reduce-scatter.8.cloned.1.call-start = ((), (), s32[]{:S(2)}) async-start(), calls=%async_computation.11 | async-start | bytes 3981312 | tf_op jit(solution)/shard_map/reduce_scatter | solution.py:312
  375.2 6.4 copy-start.9
  384.0 11.6 %slice-start = ((s8[12582912]{0:T(1024)(128)(4,1)}), s8[4194304]{0:T(1024)(128)(4,1)S(1)}, s32[]{:S(2)}) async-start(s8[12582912]{0:T(1024)(128)(4,1)} %bitcast.162), calls=%async_computation.16 | async-start | bytes 8388608 | tf_op jit(solution)/shard_map/while
  384.0 11.5 %slice-start.1 = ((s8[12582912]{0:T(1024)(128)(4,1)}), s8[4194304]{0:T(1024)(128)(4,1)S(1)}, s32[]{:S(2)}) async-start(s8[12582912]{0:T(1024)(128)(4,1)} %bitcast.162), calls=%async_computation.17 | async-start | bytes 8388608 | tf_op jit(solution)/shard_map/while
  384.0 12.8 %slice-start.2 = ((s8[12582912]{0:T(1024)(128)(4,1)}), s8[4194304]{0:T(1024)(128)(4,1)S(1)}, s32[]{:S(2)}) async-start(s8[12582912]{0:T(1024)(128)(4,1)} %bitcast.162), calls=%async_computation.18 | async-start | bytes 8388608 | tf_op jit(solution)/shard_map/while
  413.7 6.4 copy-start.9
  422.5 11.5 %slice-start = ((s8[12582912]{0:T(1024)(128)(4,1)}), s8[4194304]{0:T(1024)(128)(4,1)S(1)}, s32[]{:S(2)}) async-start(s8[12582912]{0:T(1024)(128)(4,1)} %bitcast.162), calls=%async_computation.16 | async-start | bytes 8388608 | tf_op jit(solution)/shard_map/while
  422.5 11.5 %slice-start.1 = ((s8[12582912]{0:T(1024)(128)(4,1)}), s8[4194304]{0:T(1024)(128)(4,1)S(1)}, s32[]{:S(2)}) async-start(s8[12582912]{0:T(1024)(128)(4,1)} %bitcast.162), calls=%async_computation.17 | async-start | bytes 8388608 | tf_op jit(solution)/shard_map/while
  422.6 12.7 %slice-start.2 = ((s8[12582912]{0:T(1024)(128)(4,1)}), s8[4194304]{0:T(1024)(128)(4,1)S(1)}, s32[]{:S(2)}) async-start(s8[12582912]{0:T(1024)(128)(4,1)} %bitcast.162), calls=%async_computation.18 | async-start | bytes 8388608 | tf_op jit(solution)/shard_map/while
  459.8 1.9 copy-start.1
  459.8 1.9 copy-start.25
  459.8 1.9 copy-start.27
  459.8 1.9 copy-start.36
  459.8 1.9 copy-start.43
  459.8 1.9 copy-start.50
  459.8 176.7 %reduce-scatter.14.cloned.1.call-start = ((), (), s32[]{:S(2)}) async-start(), calls=%async_computation.14 | async-start | bytes 5308416 | tf_op jit(solution)/shard_map/reduce_scatter | solution.py:327
  472.9 262.4 %reduce-scatter.12.cloned.1.call-start = ((), (), s32[]{:S(2)}) async-start(), calls=%async_computation.13 | async-start | bytes 5308416 | tf_op jit(solution)/shard_map/reduce_scatter | solution.py:324
  484.3 9.2 %copy-start.23 = (f32[768]{0:T(1024)S(1)}, f32[768]{0:T(1024)}, u32[]{:S(2)}) copy-start(f32[768]{0:T(1024)} %copy-done.22) | copy-start | bytes 9220
  484.3 9.2 %copy-start.29 = (s32[2,512]{1,0:T(2,128)S(1)}, s32[2,512]{1,0:T(2,128)}, u32[]{:S(2)}) copy-start(s32[2,512]{1,0:T(2,128)} %param.33) | copy-start | bytes 12292
  484.3 318.7 %reduce-scatter.6.cloned.1.call-start = ((), (), s32[]{:S(2)}) async-start(), calls=%async_computation.10 | async-start | bytes 1327104 | tf_op jit(solution)/shard_map/reduce_scatter | solution.py:309
  484.9 8.6 copy-start.5
  484.9 8.6 copy-start.31
  493.6 3.0 copy-start.7
  493.6 46.7 %copy-start.16 = (bf16[2,128,768]{2,1,0:T(8,128)(2,1)S(1)}, bf16[2,128,768]{2,1,0:T(8,128)(2,1)}, u32[]{:S(2)}) copy-start(bf16[2,128,768]{2,1,0:T(8,128)(2,1)} %copy-done.15) | copy-start | bytes 1179652
  540.2 55.1 %copy-start.37 = (f32[2,512]{1,0:T(2,128)S(1)}, f32[2,512]{1,0:T(2,128)}, u32[]{:S(2)}) copy-start(f32[2,512]{1,0:T(2,128)} %copy-done.35) | copy-start | bytes 12292
  541.8 309.4 %all-reduce.18.cloned.1.call-start = ((), (), s32[]{:S(2)}) async-start(), calls=%async_computation.15 | async-start | bytes 3538944 | tf_op jit(solution)/shard_map/psum | solution.py:339
  595.4 140.0 %copy-start.18 = (bf16[2,128,768]{2,1,0:T(8,128)(2,1)S(1)}, bf16[2,128,768]{2,1,0:T(8,128)(2,1)}, u32[]{:S(2)}) copy-start(bf16[2,128,768]{2,1,0:T(8,128)(2,1)} %copy-done.17) | copy-start | bytes 1179652
  597.6 139.6 %copy-start.8 = (f32[2,512,768]{2,1,0:T(8,128)S(1)}, f32[2,512,768]{2,1,0:T(8,128)}, u32[]{:S(2)}) copy-start(f32[2,512,768]{2,1,0:T(8,128)} %copy-done.7) | copy-start | bytes 9437188
  851.2 4.4 copy-start.19
  851.2 5.4 copy-start.20
  (6 other events, 4.2 us)
Sparse Core Ops, SparseCore 0:
  10.2 44.0 all-gather.6
  56.5 64.8 all-gather.8
  123.5 39.6 all-gather.10
  165.3 78.6 all-gather.12
  246.0 78.0 all-gather.14
  368.9 62.1 reduce-scatter.9
  460.0 77.3 reduce-scatter.7
  541.0 95.5 reduce-scatter.13
  640.2 95.1 reduce-scatter.11
  739.1 63.7 reduce-scatter.5
  805.6 45.5 all-reduce.17
